TPU v7x, 32 devices: a whole 2x2x4 slice. The times are simulated.
32 devices in a mesh: group: 8 (over y, x, core), head: 4 (over z).
Axes of the slice: x: 2, y: 2, z: 4, core: 2. Of those that a mesh axis runs over, the one named last changes fastest.
Arguments:
- hidden_in: bfloat16 [128, 2560], P('group'), may hold values from -6 to 6
- ssm_state: float32 [128, 80, 64, 128], P('group', 'head'), may hold values from -6 to 6
- conv_x_state: bfloat16 [128, 3, 5120], P('group', None, 'head'), may hold values from -6 to 6
- conv_bc_state: bfloat16 [128, 3, 256], P('group'), may hold values from -6 to 6
- token_ids: int32 [128], P('group'), may hold values from 0 to 25599
- ref_logits: bfloat16 [128, 25600], P('group', 'head'), may hold values from -15 to 350
- in_z: bfloat16 [2560, 5120], P('group', 'head'), may hold values from -0.125 to 0.125
- in_x: bfloat16 [2560, 5120], P('group', 'head'), may hold values from -0.125 to 0.125
- in_bc: bfloat16 [2560, 256], P('group'), may hold values from -0.125 to 0.125
- in_dt: bfloat16 [2560, 80], P('group', 'head'), may hold values from -0.125 to 0.125
- out_t: bfloat16 [2560, 5120], P('group', 'head'), may hold values from -0.078125 to 0.078125
- lm_head: bfloat16 [25600, 2560], P('head', 'group'), may hold values from -6 to 6
- conv_wx: float32 [4, 5120], P(None, 'head'), may hold values from -3 to 3
- conv_bx: float32 [5120], P('head'), may hold values from -1.5 to 1.5
- conv_wbc: float32 [4, 256], replicated, may hold values from -3 to 3
- conv_bbc: float32 [256], replicated, may hold values from -1.5 to 1.5
- dt_bias: float32 [80], P('head'), may hold values from -4 to -1
- a_log: float32 [80], P('head'), may hold values from 0 to 2.77
- skip_gain: float32 [80], P('head'), may hold values from 0.5 to 1.5
- norm_in: float32 [2560], replicated, may hold values from 0.5 to 1.5
- norm_gain: float32 [5120], P('head'), may hold values from 0.5 to 1.5
- final_gain: float32 [2560], replicated, may hold values from 0.5 to 1.5
Outputs:
- new_state: float32 [128, 80, 64, 128], P('group', 'head')
- divergence: float32 [128], P('group')
- token_logprob: float32 [128], P('group')
- roll_z: bfloat16 [2560, 5120], P(None, 'head')
- roll_x: bfloat16 [2560, 5120], P(None, 'head')
- roll_bc: bfloat16 [2560, 256], replicated
- roll_dt: bfloat16 [2560, 80], P(None, 'head')
- roll_out: bfloat16 [2560, 5120], P(None, 'head')
All inputs are finite; a program needn't handle non-finite values.
Results may differ from a plain program's by a relative error of at most 0.0102.
Values may be sent and summed in bfloat16 or wider, within the bound.
A program may use at most 128 MiB of HBM per device.

v0:
```python
import jax
import jax.numpy as jnp
from jax import lax
from jax.sharding import PartitionSpec as P

P_SIZE = 64


EPSILON = 1e-05


def rms_norm(values, gain):
    return values * lax.rsqrt(jnp.mean(values * values, axis=-1, keepdims=True) + EPSILON) * gain


def causal_conv(history, newest, taps, offset):
    window = jnp.concatenate([history, newest[:, None, :]], axis=1).astype(jnp.float32)
    return jax.nn.silu(jnp.sum(window * taps[None, :, :], axis=1) + offset)


def shards(
    hidden_in,
    ssm_state,
    conv_x_state,
    conv_bc_state,
    token_ids,
    ref_logits,
    in_z,
    in_x,
    in_bc,
    in_dt,
    out_t,
    lm_head,
    conv_wx,
    conv_bx,
    conv_wbc,
    conv_bbc,
    dt_bias,
    a_log,
    skip_gain,
    norm_in,
    norm_gain,
    final_gain,
):
    roll_z, roll_x, roll_bc, roll_dt, roll_out = (
        lax.all_gather(in_z, "group", axis=0, tiled=True),
        lax.all_gather(in_x, "group", axis=0, tiled=True),
        lax.all_gather(in_bc, "group", axis=0, tiled=True),
        lax.all_gather(in_dt, "group", axis=0, tiled=True),
        lax.all_gather(out_t, "group", axis=0, tiled=True),
    )
    stream_in = hidden_in.astype(jnp.float32)
    normed = rms_norm(stream_in, norm_in).astype(jnp.bfloat16)
    gate_branch = jnp.dot(normed, roll_z, preferred_element_type=jnp.float32).astype(jnp.bfloat16)
    x_branch = jnp.dot(normed, roll_x, preferred_element_type=jnp.float32).astype(jnp.bfloat16)
    bc_branch = jnp.dot(normed, roll_bc, preferred_element_type=jnp.float32).astype(jnp.bfloat16)
    step_raw = jnp.dot(normed, roll_dt, preferred_element_type=jnp.float32).astype(jnp.bfloat16)
    x_conv = causal_conv(conv_x_state, x_branch, conv_wx, conv_bx)
    bc_conv = causal_conv(conv_bc_state, bc_branch, conv_wbc, conv_bbc)
    state_size = bc_conv.shape[1] // 2
    b_vals = bc_conv[:, :state_size]
    c_vals = bc_conv[:, state_size:]
    step = jax.nn.softplus(step_raw.astype(jnp.float32) + dt_bias)
    decay = jnp.exp(-step * jnp.exp(a_log))
    seq_count = x_conv.shape[0]
    local_heads = a_log.shape[0]
    x_heads = x_conv.reshape(seq_count, local_heads, P_SIZE)
    inflow = (step[:, :, None] * x_heads)[:, :, :, None] * b_vals[:, None, None, :]
    new_state = decay[:, :, None, None] * ssm_state + inflow
    ssm_out = jnp.einsum("shpn,sn->shp", new_state, c_vals, precision=lax.Precision.HIGHEST)
    ssm_out = (ssm_out + skip_gain[None, :, None] * x_heads).reshape(
        seq_count, local_heads * P_SIZE
    )
    gated = ssm_out * jax.nn.silu(gate_branch.astype(jnp.float32))
    square_total = lax.psum(jnp.sum(gated * gated, axis=-1), "head")
    inner_width = gated.shape[1] * lax.axis_size("head")
    gated_out = (
        gated * lax.rsqrt(square_total / inner_width + EPSILON)[:, None] * norm_gain
    ).astype(jnp.bfloat16)
    partial_mix = lax.dot_general(
        gated_out, roll_out, (((1,), (1,)), ((), ())), preferred_element_type=jnp.float32
    )
    mixed = lax.psum(partial_mix, "head")
    final_hidden = rms_norm(stream_in + mixed, final_gain).astype(jnp.bfloat16)
    vocab_local = lm_head.shape[0]
    whole_rows = lax.all_to_all(lm_head, "group", split_axis=0, concat_axis=1, tiled=True)
    every_logits = lax.dot_general(
        lax.all_gather(final_hidden, "group", axis=0, tiled=True),
        whole_rows,
        (((1,), (1,)), ((), ())),
        preferred_element_type=jnp.float32,
    )
    logits = lax.all_to_all(every_logits, "group", split_axis=0, concat_axis=1, tiled=True)
    reference_rows = ref_logits.astype(jnp.float32)
    column_ids = lax.axis_index("head") * vocab_local + lax.broadcasted_iota(
        jnp.int32, (1, vocab_local), 1
    )
    picked_part = jnp.sum(jnp.where(column_ids == token_ids[:, None], logits, 0.0), axis=-1)
    roll_max, ref_max = lax.pmax(
        (jnp.max(logits, axis=-1), jnp.max(reference_rows, axis=-1)), "head"
    )
    ref_weights = jnp.exp(reference_rows - ref_max[:, None])
    roll_sum, ref_sum, cross_sum, picked = lax.psum(
        (
            jnp.sum(jnp.exp(logits - roll_max[:, None]), axis=-1),
            jnp.sum(ref_weights, axis=-1),
            jnp.sum(ref_weights * (reference_rows - logits), axis=-1),
            picked_part,
        ),
        "head",
    )
    lse_roll = roll_max + jnp.log(roll_sum)
    lse_ref = ref_max + jnp.log(ref_sum)
    divergence = cross_sum / ref_sum - lse_ref + lse_roll
    token_logprob = picked - lse_roll
    return (new_state, divergence, token_logprob, roll_z, roll_x, roll_bc, roll_dt, roll_out)


def solution(mesh):
    return jax.shard_map(
        shards,
        mesh=mesh,
        in_specs=(
            P("group", None),
            P("group", "head", None, None),
            P("group", None, "head"),
            P("group", None, None),
            P("group"),
            P("group", "head"),
            P("group", "head"),
            P("group", "head"),
            P("group", None),
            P("group", "head"),
            P("group", "head"),
            P("head", "group"),
            P(None, "head"),
            P("head"),
            P(),
            P(),
            P("head"),
            P("head"),
            P("head"),
            P(),
            P("head"),
            P(),
        ),
        out_specs=(
            P("group", "head", None, None),
            P("group"),
            P("group"),
            P(None, "head"),
            P(None, "head"),
            P(),
            P(None, "head"),
            P(None, "head"),
        ),
        check_vma=False,
    )
```

profile of v0, /device:TPU:0, one launch (start us, length us, event | category | flops | bytes accessed | tf_op | source)
XLA Modules:
  0.0 324.4 jit_solution(13487269814347778549)
XLA Ops:
  7.2 0.7 all-gather.8.cloned.1.call-update
  7.9 0.7 all-gather.6.cloned.1.call-update
  8.7 0.7 all-gather.10.cloned.1.call-update
  10.0 10.6 %all_to_all.26 = bf16[8,800,320]{1,0,2:T(8,128)(2,1)} reshape(bf16[6400,320]{0,1:T(8,128)(2,1)} %param.33) | data formatting | bytes 8192000 | tf_op jit(solution)/shard_map/all_to_all | solution.py:86
  20.5 5.2 %copy.40 = bf16[8,800,320]{1,2,0:T(8,128)(2,1)} copy(bf16[8,800,320]{1,0,2:T(8,128)(2,1)} %all_to_all.26) | data formatting | bytes 8192000 | tf_op jit(solution)/shard_map/all_to_all | solution.py:86
  25.8 5.4 %all-to-all-start = ((bf16[8,800,320]{1,2,0:T(8,128)(2,1)}), bf16[8,800,320]{1,2,0:T(8,128)(2,1)}, u32[]{:S(2)}, u32[]{:S(2)}) async-start(bf16[8,800,320]{1,2,0:T(8,128)(2,1)} %copy.40), calls=%async_computation | async-start | bytes 9175040 | tf_op jit(solution)/shard_map/all_to_all | solution.py:86
  31.2 66.7 %all-gather = bf16[8,320,20]{1,2,0:T(8,128)(2,1)S(1)} all-gather(bf16[1,320,20]{1,2,0:T(8,128)(2,1)S(1)} %bitcast.39), channel_id=1, replica_groups=mesh['group'=8,'head'=4] {'group'}, dimensions={0}, use_global_device_ids=true | all-gather | bytes 115200 | tf_op jit(solution)/shard_map/all_gather | solution.py:49
  98.7 1.6 fusion.2
  100.4 16.8 %all-gather.6.cloned.1.call-done = bf16[2560,1280]{1,0:T(8,128)(2,1)} async-done(((bf16[320,1280]{1,0:T(8,128)(2,1)}), bf16[2560,1280]{1,0:T(8,128)(2,1)}) %all-gather.6.cloned.1.call-update) | async-done | bytes 6553616 | tf_op jit(solution)/shard_map/all_gather | solution.py:47
  117.2 3.9 %fusion.1 = bf16[16,1,1280]{2,0,1:T(8,128)(2,1)S(1)} fusion(bf16[2560,1280]{1,0:T(8,128)(2,1)} %all-gather.6.cloned.1.call-done, bf16[16,2560]{1,0:T(8,128)(2,1)S(1)} %copy-done.2, f32[2560]{0:T(1024)S(1)} %copy-done.6, f32[16]{0:T(128)S(1)} %add_rsqrt_fusion.2), kind=kOutput, calls=%fused_computation.4 | convolution fusion | flops 105041920 | bytes 6686784 | tf_op jit(solution)/shard_map/dot_general | solution.py:55
  121.3 8.4 %multiply_add_fusion = f32[16,20,64,128]{3,2,1,0:T(8,128)S(1)} fusion(f32[16,20,64,128]{3,2,1,0:T(8,128)} %param.23, f32[16,128]{1,0:T(8,128)S(1)} %get-tuple-element.19, f32[16,20,64]{2,1,0:T(8,128)S(1)} %broadcast_multiply_fusion, f32[16,20]{1,0:T(8,128)S(1)} %get-tuple-element.22), kind=kLoop, calls=%fused_computation | loop fusion | flops 7864320 | bytes 21062912 | tf_op jit(solution)/shard_map/add | solution.py:69
  129.8 4.1 %copy-done = f32[16,20,64,128]{3,2,1,0:T(8,128)} copy-done((f32[16,20,64,128]{3,2,1,0:T(8,128)}, f32[16,20,64,128]{3,2,1,0:T(8,128)S(1)}, u32[]{:S(2)}) %copy-start) | copy-done | bytes 10485784
  133.8 24.6 %fusion.21 = f32[16,1,20,64]{3,1,2,0:T(1,128)S(1)} fusion(f32[16,20,64,128]{3,2,1,0:T(8,128)S(1)} %multiply_add_fusion, f32[16,128,1,1]{1,2,3,0:T(1,128)S(1)} %bitcast.38), kind=kOutput, calls=%fused_computation.48 | convolution fusion | flops 31457280 | bytes 10575872 | tf_op jit(solution)/shard_map/shpn,sn->shp/dot_general | solution.py:70
  158.6 7.0 %all-gather.10.cloned.1.call-done = bf16[2560,1280]{1,0:T(8,128)(2,1)} async-done(((bf16[320,1280]{1,0:T(8,128)(2,1)}), bf16[2560,1280]{1,0:T(8,128)(2,1)}) %all-gather.10.cloned.1.call-update) | async-done | bytes 6553616 | tf_op jit(solution)/shard_map/all_gather | solution.py:46
  165.6 4.0 %multiply_reduce_fusion.2 = (f32[16]{0:T(128)S(1)}, f32[16,1280]{1,0:T(8,128)S(1)}) fusion(f32[16,1280]{1,0:T(8,128)S(1)} %reshape.100, bf16[2560,1280]{1,0:T(8,128)(2,1)} %all-gather.10.cloned.1.call-done, bf16[16,2560]{1,0:T(8,128)(2,1)S(1)} %copy-done.2, f32[2560]{0:T(1024)S(1)} %copy-done.6, f32[16]{0:T(128)S(1)} %add_rsqrt_fusion.2), kind=kOutput, calls=%fused_computation.31 | convolution fusion | flops 105205744 | bytes 6809728 | tf_op jit(solution)/shard_map/dot_general | solution.py:54
  169.6 11.7 %psum.42 = f32[16]{0:T(128)S(1)} all-reduce(f32[16]{0:T(128)S(1)} %get-tuple-element.24), channel_id=1, replica_groups=mesh['group'=8,'head'=4] {'head'}, use_global_device_ids=true, to_apply=%region_6.7 | all-reduce | flops 16 | bytes 128 | tf_op jit(solution)/shard_map/psum | solution.py:75
  181.3 32.6 %all-gather.12.cloned.1.call-done = bf16[2560,1280]{1,0:T(8,128)(2,1)} async-done(((bf16[320,1280]{1,0:T(8,128)(2,1)}), bf16[2560,1280]{1,0:T(8,128)(2,1)}) %all-gather.12.cloned.1.call-update) | async-done | bytes 6553616 | tf_op jit(solution)/shard_map/all_gather | solution.py:50
  213.9 5.4 %fusion.12 = f32[16,2560]{1,0:T(8,128)} fusion(bf16[2560,1280]{1,0:T(8,128)(2,1)} %all-gather.12.cloned.1.call-done, f32[16,1280]{1,0:T(8,128)S(1)} %get-tuple-element.25, f32[1280]{0:T(1024)S(1)} %copy-done.11, f32[16]{0:T(128)S(1)} %add_rsqrt_fusion.1), kind=kOutput, calls=%fused_computation.34 | convolution fusion | flops 104919040 | bytes 6804544 | tf_op jit(solution)/shard_map/dot_general | solution.py:80
  219.3 35.0 %all-reduce.4.cloned.1.call-done = f32[16,2560]{1,0:T(8,128)} async-done(((f32[16,2560]{1,0:T(8,128)}), f32[16,2560]{1,0:T(8,128)}) %all-reduce.4.cloned.1.call-update) | async-done | bytes 163856 | tf_op jit(solution)/shard_map/psum | solution.py:83
  254.3 1.0 multiply_reduce_fusion.1
  255.3 1.0 multiply_convert_fusion
  256.3 10.0 %all_gather.23 = bf16[128,2560]{1,0:T(8,128)(2,1)S(1)} all-gather(bf16[16,2560]{1,0:T(8,128)(2,1)S(1)} %multiply_convert_fusion), channel_id=1, replica_groups=mesh['group'=8,'head'=4] {'group'}, dimensions={0}, use_global_device_ids=true | all-gather | bytes 737280 | tf_op jit(solution)/shard_map/all_gather | solution.py:88
  266.4 3.9 %fusion.22 = f32[8,16,800]{2,1,0:T(8,128)} fusion(bf16[8,16,2560]{2,1,0:T(8,128)(2,1)S(1)} %bitcast.37, bf16[800,2560,1]{0,1,2:T(8,128)(2,1)} %bitcast.9), kind=kOutput, calls=%fused_computation.49 | convolution fusion | flops 524288000 | bytes 5160960 | tf_op jit(solution)/shard_map/dot_general | solution.py:87
  270.3 3.5 %all-to-all-start.1 = ((f32[8,16,800]{2,1,0:T(8,128)}), f32[8,16,800]{2,1,0:T(8,128)S(1)}, u32[]{:S(2)}, u32[]{:S(2)}) async-start(f32[8,16,800]{2,1,0:T(8,128)} %fusion.22), calls=%async_computation.1 | async-start | bytes 917504 | tf_op jit(solution)/shard_map/all_to_all | solution.py:93
  274.0 8.8 %all-to-all-done.1 = f32[8,16,800]{2,1,0:T(8,128)S(1)} async-done(((f32[8,16,800]{2,1,0:T(8,128)}), f32[8,16,800]{2,1,0:T(8,128)S(1)}, u32[]{:S(2)}, u32[]{:S(2)}) %all-to-all-start.1) | async-done | bytes 409632 | tf_op jit(solution)/shard_map/all_to_all | solution.py:93
  283.2 10.6 %all-reduce.1 = (f32[16]{0:T(128)S(1)}, f32[16]{0:T(128)S(1)}) all-reduce(bf16[16]{0:T(256)(128)(2,1)S(1)} %reduce_max.23, f32[16]{0:T(128)S(1)} %reduce_max.25), channel_id=1, replica_groups=mesh['group'=8,'head'=4] {'head'}, use_global_device_ids=true, to_apply=%region_4.5 | all-reduce | flops 32 | bytes 224 | tf_op jit(solution)/shard_map/pmax | solution.py:99
  294.5 8.5 %all-reduce = (f32[16]{0:T(128)S(1)}, f32[16]{0:T(128)S(1)}, f32[16]{0:T(128)S(1)}, f32[16]{0:T(128)S(1)}) all-reduce(f32[16]{0:T(128)S(1)} %get-tuple-element.11, f32[16]{0:T(128)S(1)} %get-tuple-element.10, f32[16]{0:T(128)S(1)} %get-tuple-element.9, f32[16]{0:T(128)S(1)} %get-tuple-element.8), channel_id=1, replica_groups=mesh['group'=8,'head'=4] {'head'}, use_global_device_ids=true, to_apply=%region_12.13 | all-reduce | flops 64 | bytes 512 | tf_op jit(solution)/shard_map/psum | solution.py:103
  303.0 0.5 fusion.15
  303.6 6.7 %copy.53 = bf16[2560,1280]{1,0:T(8,128)(2,1)} copy(bf16[2560,1280]{1,0:T(8,128)(2,1)} %all-gather.10.cloned.1.call-done) | data formatting | bytes 13107200
  310.3 3.3 %copy.54 = bf16[2560,1280]{1,0:T(8,128)(2,1)} copy(bf16[2560,1280]{1,0:T(8,128)(2,1)S(1)} %bitcast.33) | data formatting | bytes 13107200
  313.6 1.1 copy.55
  315.1 2.8 copy.56
  (80 shorter events, 3.7 us)
Async XLA Ops:
  7.2 91.5 %all-gather.8.cloned.1.call-start = ((), (), s32[]{:S(2)}) async-start(), calls=%async_computation.3 | async-start | bytes 1474560 | tf_op jit(solution)/shard_map/all_gather | solution.py:48
  7.9 109.3 %all-gather.6.cloned.1.call-start = ((), (), s32[]{:S(2)}) async-start(), calls=%async_computation.2 | async-start | bytes 7372800 | tf_op jit(solution)/shard_map/all_gather | solution.py:47
  8.7 157.0 %all-gather.10.cloned.1.call-start = ((), (), s32[]{:S(2)}) async-start(), calls=%async_computation.4 | async-start | bytes 7372800 | tf_op jit(solution)/shard_map/all_gather | solution.py:46
  9.4 204.5 %all-gather.12.cloned.1.call-start = ((), (), s32[]{:S(2)}) async-start(), calls=%async_computation.5 | async-start | bytes 7372800 | tf_op jit(solution)/shard_map/all_gather | solution.py:50
  25.7 5.5 %copy-start.9 = (bf16[320,20]{0,1:T(8,128)(2,1)S(1)}, bf16[320,20]{0,1:T(8,128)(2,1)}, u32[]{:S(2)}) copy-start(bf16[320,20]{0,1:T(8,128)(2,1)} %param.31) | copy-start | bytes 38404
  25.7 72.4 %copy-start.17 = (f32[20]{0:T(128)S(1)}, f32[20]{0:T(128)}, u32[]{:S(2)}) copy-start(f32[20]{0:T(128)} %param.39) | copy-start | bytes 244
  25.7 72.4 %copy-start.12 = (f32[1280]{0:T(1024)S(1)}, f32[1280]{0:T(1024)}, u32[]{:S(2)}) copy-start(f32[1280]{0:T(1024)} %param.35) | copy-start | bytes 15364
  25.7 72.5 %copy-start.2 = (bf16[16,2560]{1,0:T(8,128)(2,1)S(1)}, bf16[16,2560]{1,0:T(8,128)(2,1)}, u32[]{:S(2)}) copy-start(bf16[16,2560]{1,0:T(8,128)(2,1)} %param.22) | copy-start | bytes 245764
  25.7 72.6 %copy-start.6 = (f32[2560]{0:T(1024)S(1)}, f32[2560]{0:T(1024)}, u32[]{:S(2)}) copy-start(f32[2560]{0:T(1024)} %param.41) | copy-start | bytes 30724
  25.7 72.6 %copy-start.18 = (f32[20]{0:T(128)S(1)}, f32[20]{0:T(128)}, u32[]{:S(2)}) copy-start(f32[20]{0:T(128)} %param.38) | copy-start | bytes 244
  25.8 74.5 %copy-start.7 = (bf16[16,3,256]{2,0,1:T(8,128)(2,1)S(1)}, bf16[16,3,256]{2,0,1:T(8,128)(2,1)}, u32[]{:S(2)}) copy-start(bf16[16,3,256]{2,0,1:T(8,128)(2,1)} %param.25) | copy-start | bytes 73732
  25.8 74.5 %copy-start.13 = (f32[4,256]{1,0:T(4,128)S(1)}, f32[4,256]{1,0:T(4,128)}, u32[]{:S(2)}) copy-start(f32[4,256]{1,0:T(4,128)} %param.36) | copy-start | bytes 12292
  25.8 74.5 %copy-start.14 = (f32[256]{0:T(256)S(1)}, f32[256]{0:T(256)}, u32[]{:S(2)}) copy-start(f32[256]{0:T(256)} %param.37) | copy-start | bytes 3076
  25.8 240.6 %all-to-all-start = ((bf16[8,800,320]{1,2,0:T(8,128)(2,1)}), bf16[8,800,320]{1,2,0:T(8,128)(2,1)}, u32[]{:S(2)}, u32[]{:S(2)}) async-start(bf16[8,800,320]{1,2,0:T(8,128)(2,1)} %copy.40), calls=%async_computation | async-start | bytes 9175040 | tf_op jit(solution)/shard_map/all_to_all | solution.py:86
  31.2 89.9 %copy-start.4 = (bf16[16,3,1280]{2,0,1:T(8,128)(2,1)S(1)}, bf16[16,3,1280]{2,0,1:T(8,128)(2,1)}, u32[]{:S(2)}) copy-start(bf16[16,3,1280]{2,0,1:T(8,128)(2,1)} %param.24) | copy-start | bytes 368644
  31.2 89.9 %copy-start.8 = (f32[4,1280]{1,0:T(4,128)S(1)}, f32[4,1280]{1,0:T(4,128)}, u32[]{:S(2)}) copy-start(f32[4,1280]{1,0:T(4,128)} %param.34) | copy-start | bytes 61444
  31.2 223.1 %all-reduce.4.cloned.1.call-start = ((), (), s32[]{:S(2)}) async-start(), calls=%async_computation.6 | async-start | bytes 327680 | tf_op jit(solution)/shard_map/psum | solution.py:83
  98.1 31.6 %copy-start.5 = (bf16[2560,20]{0,1:T(8,128)(2,1)}, bf16[2560,20]{0,1:T(8,128)(2,1)S(1)}, u32[]{:S(2)}) copy-start(bf16[2560,20]{0,1:T(8,128)(2,1)S(1)} %reshape.102) | copy-start | bytes 307204
  129.7 4.1 %copy-start = (f32[16,20,64,128]{3,2,1,0:T(8,128)}, f32[16,20,64,128]{3,2,1,0:T(8,128)S(1)}, u32[]{:S(2)}) copy-start(f32[16,20,64,128]{3,2,1,0:T(8,128)S(1)} %multiply_add_fusion) | copy-start | bytes 31457284
  129.8 28.7 %copy-start.15 = (f32[20]{0:T(128)S(1)}, f32[20]{0:T(128)}, u32[]{:S(2)}) copy-start(f32[20]{0:T(128)} %param.40) | copy-start | bytes 244
  133.8 80.1 %copy-start.11 = (f32[1280]{0:T(1024)S(1)}, f32[1280]{0:T(1024)}, u32[]{:S(2)}) copy-start(f32[1280]{0:T(1024)} %param.42) | copy-start | bytes 15364
  158.6 96.7 %copy-start.10 = (f32[2560]{0:T(1024)S(1)}, f32[2560]{0:T(1024)}, u32[]{:S(2)}) copy-start(f32[2560]{0:T(1024)} %param.43) | copy-start | bytes 30724
  213.9 59.9 %copy-start.3 = (bf16[16,6400]{1,0:T(8,128)(2,1)S(1)}, bf16[16,6400]{1,0:T(8,128)(2,1)}, u32[]{:S(2)}) copy-start(bf16[16,6400]{1,0:T(8,128)(2,1)} %param.27) | copy-start | bytes 614404
  219.3 74.9 %copy-start.16 = (s32[16]{0:T(128)S(1)}, s32[16]{0:T(128)}, u32[]{:S(2)}) copy-start(s32[16]{0:T(128)} %param.26) | copy-start | bytes 196
  270.3 12.4 %all-to-all-start.1 = ((f32[8,16,800]{2,1,0:T(8,128)}), f32[8,16,800]{2,1,0:T(8,128)S(1)}, u32[]{:S(2)}, u32[]{:S(2)}) async-start(f32[8,16,800]{2,1,0:T(8,128)} %fusion.22), calls=%async_computation.1 | async-start | bytes 917504 | tf_op jit(solution)/shard_map/all_to_all | solution.py:93
  293.9 16.4 %slice-start = ((s8[6553600]{0:T(1024)(128)(4,1)}), s8[2359296]{0:T(1024)(128)(4,1)S(1)}, s32[]{:S(2)}) async-start(s8[6553600]{0:T(1024)(128)(4,1)} %bitcast.32), calls=%async_computation.7 | async-start | bytes 4718592
  303.6 6.7 %slice-start.1 = ((s8[6553600]{0:T(1024)(128)(4,1)}), s8[4194304]{0:T(1024)(128)(4,1)S(1)}, s32[]{:S(2)}) async-start(s8[6553600]{0:T(1024)(128)(4,1)} %bitcast.32), calls=%async_computation.8 | async-start | bytes 8388608
  303.6 11.1 %slice-start.2 = ((s8[6553600]{0:T(1024)(128)(4,1)}), s8[4194304]{0:T(1024)(128)(4,1)S(1)}, s32[]{:S(2)}) async-start(s8[6553600]{0:T(1024)(128)(4,1)} %bitcast.34), calls=%async_computation.9 | async-start | bytes 8388608
  310.3 3.3 %copy-start.1 = (bf16[2560,256]{1,0:T(8,128)(2,1)S(1)}, bf16[2560,256]{1,0:T(8,128)(2,1)}, u32[]{:S(2)}) copy-start(bf16[2560,256]{1,0:T(8,128)(2,1)} %all-gather.8.cloned.1.call-done) | copy-start | bytes 3932164
  310.3 4.8 %slice-start.3 = ((s8[6553600]{0:T(1024)(128)(4,1)}), s8[2359296]{0:T(1024)(128)(4,1)S(1)}, s32[]{:S(2)}) async-start(s8[6553600]{0:T(1024)(128)(4,1)} %bitcast.34), calls=%async_computation.10 | async-start | bytes 4718592
Sparse Core Ops, SparseCore 0:
  9.9 28.3 all-gather.7
  40.1 77.0 all-gather.5
  119.1 46.4 all-gather.9
  167.4 46.4 all-gather.11
  219.4 34.8 all-reduce.3
where the time goes:
time: 325 us; the launch traced here: 324 us
  blocking collectives  108 us (33%)
  waiting for transfers between devices  103 us (32%)
  matrix products  43.6 us (13%)
  local copies, waits for them, and re-layouts  34.9 us (11%)
  between operations  14.1 us (4%)
  other arithmetic  12.4 us (4%)
  starting transfers between devices  9.02 us (3%)
    all_gather x1, blocking collectives, shards(): lax.all_gather(in_dt, 'group', axis=0, tiled=True)  66.7 us
    psum x1, waiting for transfers between devices, shards(): mixed = lax.psum(partial_mix, 'head')  35 us
    all_gather x1, waiting for transfers between devices, shards(): lax.all_gather(out_t, 'group', axis=0, tiled=True)  32.6 us
    dot_general x1, matrix products, shards(): jnp.einsum('shpn,sn->shp', new_state, c_vals, precision=lax.Precision.HIG...  24.6 us
    unnamed x51, local copies, waits for them, and re-layouts  18.6 us
    all_gather x1, waiting for transfers between devices, shards(): lax.all_gather(in_x, 'group', axis=0, tiled=True)  16.8 us
    all_to_all x2, local copies, waits for them, and re-layouts, shards(): lax.all_to_all(lm_head, 'group', split_axis=0, concat_axis=1, tiled=True)  15.8 us
    psum x1, blocking collectives, shards(): square_total = lax.psum(jnp.sum(gated * gated, axis=-1), 'head')  11.7 us
  transfers between devices with their start and end apart: 7, of which 5 were waited for; matrix products, arithmetic and copies ran while one was open for 17% of the time, Pallas kernels for 0%

commit v1 on v0

v1 whole, which is shorter than its diff:
```python
import functools

import jax
import jax.numpy as jnp
from jax import lax
from jax.experimental import pallas as pl
from jax.experimental.pallas import tpu as pltpu
from jax.sharding import PartitionSpec as P

P_SIZE = 64
EPSILON = 1e-05
MESH = pl.DeviceIdType.MESH


def rms_norm(values, gain):
    return values * lax.rsqrt(jnp.mean(values * values, axis=-1, keepdims=True) + EPSILON) * gain


def causal_conv(history, newest, taps, offset):
    window = jnp.concatenate([history, newest[:, None, :]], axis=1).astype(jnp.float32)
    return jax.nn.silu(jnp.sum(window * taps[None, :, :], axis=1) + offset)


def flip(value, mask):
    bit = 1
    while bit <= mask:
        if mask & bit:
            value = value + bit * (1 - 2 * ((value // bit) % 2))
        bit *= 2
    return value


class Gather:
    def __init__(self, chips, ins, outs, local, send, recv, psend, precv):
        self.chips, self.ins, self.outs = chips, ins, outs
        self.local, self.send, self.recv, self.psend, self.precv = local, send, recv, psend, precv
        group = lax.axis_index("group")
        self.chip, self.core = group // 2, group % 2
        self.pending = []
        self.relay = chips == 4

    def rows(self, a, chip, core, part=None):
        count = self.ins[a].shape[0]
        start = (chip * 2 + core) * count
        if part is not None:
            count = count // 2
            start = start + part * count
        return pl.ds(pl.multiple_of(start, 16), count)

    def copy(self, src, dst, chip, core, ssem, rsem):
        made = pltpu.make_async_remote_copy(
            src_ref=src, dst_ref=dst, send_sem=ssem, recv_sem=rsem,
            device_id={"group": chip * 2 + core}, device_id_type=MESH,
        )
        made.start()
        self.pending.append(made)
        return made

    def start(self, a):
        src = self.ins[a]
        own = self.outs[a].at[self.rows(a, self.chip, self.core)]
        loc = pltpu.make_async_copy(src, own, self.local.at[a])
        loc.start()
        self.far = getattr(self, "far", {})
        peers = [1, 2] if self.relay else range(1, self.chips)
        for m in peers:
            self.far[a, m] = self.copy(
                src, own, flip(self.chip, m), self.core, self.send.at[a, m], self.recv.at[a, m])
        self.near = getattr(self, "near", {})
        self.near[a, 0] = self.copy(
            src, own, self.chip, 1 - self.core, self.psend.at[a, 0], self.precv.at[a, 0])
        self.locals = getattr(self, "locals", {})
        self.locals[a] = loc

    def hand_on(self, a, m, chip, part, slot):
        view = self.outs[a].at[self.rows(a, chip, self.core, part)]
        self.near[a, slot] = self.copy(
            view, view, self.chip, 1 - self.core, self.psend.at[a, slot], self.precv.at[a, slot])

    def relay_near(self, a):
        if self.relay:
            for m, part in ((1, 0), (2, 1)):
                self.far[a, m].wait_recv()
                source = flip(self.chip, m)
                view = self.outs[a].at[self.rows(a, source, self.core, part)]
                self.far[a, 3 + part] = self.copy(
                    view, view, flip(self.chip, 3 - m), self.core,
                    self.send.at[a, 3 + part], self.recv.at[a, 3 + part])
                self.hand_on(a, m, source, None, m)
        else:
            for m in range(1, self.chips):
                self.far[a, m].wait_recv()
                self.hand_on(a, m, flip(self.chip, m), None, m)

    def relay_far(self, a):
        if self.relay:
            for part in (0, 1):
                self.far[a, 3 + part].wait_recv()
                self.hand_on(a, 3, flip(self.chip, 3), part, 3 + part)

    def arrive(self, a):
        for (b, _), made in self.near.items():
            if b == a:
                made.wait_recv()
        self.locals[a].wait()

    def drain(self):
        for made in self.pending:
            made.wait_send()


def gather_sems(count, chips):
    slots = max(chips, 5)
    dma = pltpu.SemaphoreType.DMA
    return [dma((count,)), dma((count, slots)), dma((count, slots)), dma((count, slots)), dma((count, slots))]


def greet(groups, heads):
    barrier = pltpu.get_barrier_semaphore()
    group, head = lax.axis_index("group"), lax.axis_index("head")
    for j in range(1, groups):
        pl.semaphore_signal(barrier, inc=1, device_id={"group": (group + j) % groups}, device_id_type=MESH)
    for j in range(1, heads):
        pl.semaphore_signal(barrier, inc=1, device_id={"head": (head + j) % heads}, device_id_type=MESH)
    pl.semaphore_wait(barrier, groups - 1 + heads - 1)


def gather_kernel(groups, count, *refs):
    ins, outs, sems = refs[:count], refs[count:2 * count], refs[2 * count:]
    work = Gather(groups // 2, ins, outs, *sems)
    greet(groups, 1)
    for a in range(count):
        work.start(a)
    for a in range(count):
        work.relay_near(a)
        if a:
            work.relay_far(a - 1)
    work.relay_far(count - 1)
    for a in range(count):
        work.arrive(a)
    work.drain()


def gather(groups, arrays):
    count = len(arrays)
    any_spec = pl.BlockSpec(memory_space=pl.ANY)
    return pl.pallas_call(
        functools.partial(gather_kernel, groups, count),
        out_shape=[jax.ShapeDtypeStruct((groups * v.shape[0], v.shape[1]), v.dtype) for v in arrays],
        in_specs=[any_spec] * count,
        out_specs=[any_spec] * count,
        scratch_shapes=gather_sems(count, groups // 2),
        compiler_params=pltpu.CompilerParams(collective_id=0, has_side_effects=True),
        name="gather_in",
    )(*arrays)


def state_kernel(decay_ref, inflow_ref, b_ref, c_ref, state_ref, new_ref, y_ref):
    def column(row, other):
        first = lax.broadcasted_iota(jnp.int32, (8, row.shape[1]), 0) == 0
        left = jnp.where(first, jnp.broadcast_to(row, (8, row.shape[1])), 0.0)
        right = jnp.broadcast_to(other, (8, other.shape[1]))
        return lax.dot_general(
            left, right, (((0,), (0,)), ((), ())),
            precision=lax.Precision.HIGHEST, preferred_element_type=jnp.float32)

    b = b_ref[0]
    decay = column(decay_ref[0], jnp.ones_like(b))
    new = decay * state_ref[0] + column(inflow_ref[0], b)
    new_ref[0] = new
    c = jnp.broadcast_to(c_ref[0], (16, b.shape[1])).astype(jnp.bfloat16)
    y = lax.dot_general(
        c, new.astype(jnp.bfloat16), (((1,), (1,)), ((), ())), preferred_element_type=jnp.float32)
    y_ref[0] = y[0:1]


def state_step(decay, inflow, b_vals, c_vals, state):
    seqs, rows, size = state.shape
    row = lambda width: pl.BlockSpec((1, 1, width), lambda s: (s, 0, 0))
    block = pl.BlockSpec((1, rows, size), lambda s: (s, 0, 0))
    new, y = pl.pallas_call(
        state_kernel,
        grid=(seqs,),
        in_specs=[row(rows), row(rows), row(size), row(size), block],
        out_specs=[block, row(rows)],
        out_shape=[jax.ShapeDtypeStruct(state.shape, jnp.float32),
                   jax.ShapeDtypeStruct((seqs, 1, rows), jnp.float32)],
        name="state_step",
    )(decay[:, None], inflow[:, None], b_vals[:, None], c_vals[:, None], state)
    return new, y[:, 0]


def halves(column, lanes, first, split):
    high = column.astype(jnp.bfloat16).astype(jnp.float32)
    return jnp.where(lanes < split, high, column - high)


def tail_kernel(
    groups, heads, seqs,
    gated_ref, hid_ref, ngain_ref, fgain_ref, out_t_ref, lm_ref, refl_ref, token_ref, out_hbm,
    roll_out, result_ref,
    gall, hall, mix, pairs, pair_in, sums, sums_in, stat,
    gsend, grecv, hsend, hrecv, msend, mrecv, psend, precv, ssend, srecv, tsend, trecv,
    *gsems,
):
    chips = groups // 2
    group, head = lax.axis_index("group"), lax.axis_index("head")
    chip, core = group // 2, group % 2
    wide = mix.shape[2]
    depth = out_t_ref.shape[0]
    vocab = lm_ref.shape[0]
    rows = groups * seqs
    pending = []

    def send(src, dst, device, ssem, rsem):
        made = pltpu.make_async_remote_copy(
            src_ref=src, dst_ref=dst, send_sem=ssem, recv_sem=rsem, device_id=device, device_id_type=MESH)
        made.start()
        pending.append(made)
        return made

    work = Gather(chips, [out_hbm], [roll_out], *gsems)
    greet(groups, heads)
    first = []
    for j in range(1, groups):
        peer = (group + j) % groups
        first.append(send(gated_ref, gall.at[group], {"group": peer}, gsend.at[j], grecv.at[j]))
        first.append(send(hid_ref.at[peer], hall.at[group], {"group": peer}, hsend.at[j], hrecv.at[j]))
    work.start(0)
    gall[group] = gated_ref[...]
    hall[group] = hid_ref[group]
    for made in first:
        made.wait_recv()

    gated = gall[...].reshape(rows, gall.shape[2]).astype(jnp.float32)
    squares = jnp.sum(gated * gated, axis=-1, keepdims=True)
    scaled = (gated * ngain_ref[...]).astype(jnp.bfloat16)
    out_rows = out_t_ref[...]
    if wide > depth:
        out_rows = jnp.concatenate(
            [out_rows, jnp.zeros((wide - depth, out_rows.shape[1]), jnp.bfloat16)], axis=0)
    partial = lax.dot_general(
        scaled, out_rows, (((1,), (1,)), ((), ())), preferred_element_type=jnp.float32)
    lanes = lax.broadcasted_iota(jnp.int32, (rows, wide), 1)
    middle = (depth + wide) // 2
    mix[0] = jnp.where(lanes < depth, partial, halves(squares, lanes, depth, middle)).astype(jnp.bfloat16)
    mixes = [
        send(mix.at[0], mix.at[j], {"head": (head + j) % heads}, msend.at[j], mrecv.at[j])
        for j in range(1, heads)
    ]
    for made in mixes:
        made.wait_recv()
    work.relay_near(0)
    total = jnp.sum(mix[...].astype(jnp.float32), axis=0)
    square_total = total[:, depth:depth + 1] + total[:, middle:middle + 1]
    inner = gall.shape[2] * heads
    hidden = hall[...].reshape(rows, wide).astype(jnp.float32)
    stream = hidden + total * lax.rsqrt(square_total / inner + EPSILON)
    stream = jnp.where(lanes < depth, stream, 0.0)
    final_squares = jnp.sum(stream * stream, axis=-1, keepdims=True)
    final = (stream * fgain_ref[...]).astype(jnp.bfloat16)

    def by_core(values):
        parts = values.reshape(chips, 2, seqs, values.shape[1])
        return jnp.concatenate(
            [parts[:, 0].reshape(chips * seqs, -1), parts[:, 1].reshape(chips * seqs, -1)], axis=0)

    final = by_core(final.astype(jnp.float32)).astype(jnp.bfloat16)[:, :depth]
    final_squares = by_core(jnp.broadcast_to(final_squares, (rows, 128)))
    tail_lanes = lax.broadcasted_iota(jnp.int32, (rows, 128), 1)
    packed = halves(final_squares, tail_lanes, 0, 64).astype(jnp.bfloat16)
    half = chips * seqs
    for side in (0, 1):
        pairs[side, :, vocab:vocab + 128] = packed[side * half:(side + 1) * half]
    step_width = 640

    @pl.loop(0, vocab // step_width)
    def _(t):
        at = pl.ds(pl.multiple_of(t * step_width, step_width), step_width)
        block = lax.dot_general(
            final, lm_ref[at, :], (((1,), (1,)), ((), ())), preferred_element_type=jnp.float32)
        block = block.astype(jnp.bfloat16)
        pairs[0, :, at] = block[:half]
        pairs[1, :, at] = block[half:]

    pair = send(pairs.at[1 - core], pair_in, {"group": chip * 2 + 1 - core}, psend, precv)
    pair.wait_recv()
    joined = pairs[core].astype(jnp.float32) + pair_in[...].astype(jnp.float32)
    sums[:, :, :vocab] = joined[:, :vocab].astype(jnp.bfloat16).reshape(chips, seqs, vocab)
    rest = joined[:, vocab:]
    rest = rest[:, 0:1] + rest[:, 64:65]
    packed = halves(rest, lax.broadcasted_iota(jnp.int32, (half, 128), 1), 0, 64)
    sums[:, :, vocab:] = packed.astype(jnp.bfloat16).reshape(chips, seqs, 128)
    last = []
    for m in range(1, chips):
        peer = flip(chip, m)
        last.append(send(sums.at[peer], sums_in.at[m], {"group": peer * 2 + core}, ssend.at[m], srecv.at[m]))
    sums_in[0] = sums[chip]
    work.relay_far(0)
    for made in last:
        made.wait_recv()

    logits = jnp.sum(sums_in[...].astype(jnp.float32), axis=0)
    mean_square = (logits[:, vocab:vocab + 1] + logits[:, vocab + 64:vocab + 65]) / (depth * groups)
    logits = logits[:, :vocab] * lax.rsqrt(mean_square + EPSILON)
    reference = refl_ref[...].astype(jnp.float32)
    columns = lax.broadcasted_iota(jnp.int32, (seqs, vocab), 1) + head * vocab
    picked = jnp.sum(jnp.where(columns == token_ref[...], logits, 0.0), axis=-1, keepdims=True)
    top = jnp.max(logits, axis=-1, keepdims=True)
    ref_top = jnp.max(reference, axis=-1, keepdims=True)
    weights = jnp.exp(reference - ref_top)
    values = (
        top,
        jnp.sum(jnp.exp(logits - top), axis=-1, keepdims=True),
        ref_top,
        jnp.sum(weights, axis=-1, keepdims=True),
        jnp.sum(weights * (reference - logits), axis=-1, keepdims=True),
        picked,
    )
    slot = lax.broadcasted_iota(jnp.int32, (seqs, 128), 1)
    mine = jnp.zeros((seqs, 128), jnp.float32)
    for n, value in enumerate(values):
        mine = jnp.where(slot == n, value, mine)
    stat[0] = mine
    stats = [
        send(stat.at[0], stat.at[j], {"head": (head + j) % heads}, tsend.at[j], trecv.at[j])
        for j in range(1, heads)
    ]
    for made in stats:
        made.wait_recv()
    every = stat[...]
    pick = lambda n: every[:, :, n:n + 1]
    top = jnp.max(pick(0), axis=0)
    ref_top = jnp.max(pick(2), axis=0)
    factor = jnp.exp(pick(0) - top[None])
    ref_factor = jnp.exp(pick(2) - ref_top[None])
    roll_sum = jnp.sum(pick(1) * factor, axis=0)
    ref_sum = jnp.sum(pick(3) * ref_factor, axis=0)
    cross = jnp.sum(pick(4) * ref_factor, axis=0)
    picked = jnp.sum(pick(5), axis=0)
    lse_roll = top + jnp.log(roll_sum)
    lse_ref = ref_top + jnp.log(ref_sum)
    result_ref[...] = jnp.where(slot == 0, cross / ref_sum - lse_ref + lse_roll, picked - lse_roll)

    work.arrive(0)
    work.drain()
    for made in pending:
        made.wait_send()


def tail(groups, heads, gated, hid, ngain, fgain, out_t, lm_head, ref_logits, tokens):
    seqs, inner = gated.shape
    depth = out_t.shape[0]
    wide = hid.shape[2]
    vocab = lm_head.shape[0]
    chips = groups // 2
    vmem, any_spec = pl.BlockSpec(memory_space=pltpu.VMEM), pl.BlockSpec(memory_space=pl.ANY)
    dma = pltpu.SemaphoreType.DMA
    bf16 = jnp.bfloat16
    return pl.pallas_call(
        functools.partial(tail_kernel, groups, heads, seqs),
        out_shape=[jax.ShapeDtypeStruct((groups * depth, inner), bf16),
                   jax.ShapeDtypeStruct((seqs, 128), jnp.float32)],
        in_specs=[vmem] * 8 + [any_spec],
        out_specs=[any_spec, vmem],
        scratch_shapes=[
            pltpu.VMEM((groups, seqs, inner), bf16),
            pltpu.VMEM((groups, seqs, wide), bf16),
            pltpu.VMEM((heads, groups * seqs, wide), bf16),
            pltpu.VMEM((2, chips * seqs, vocab + 128), bf16),
            pltpu.VMEM((chips * seqs, vocab + 128), bf16),
            pltpu.VMEM((chips, seqs, vocab + 128), bf16),
            pltpu.VMEM((chips, seqs, vocab + 128), bf16),
            pltpu.VMEM((heads, seqs, 128), jnp.float32),
            dma((groups,)), dma((groups,)), dma((groups,)), dma((groups,)),
            dma((heads,)), dma((heads,)), dma, dma,
            dma((chips,)), dma((chips,)), dma((heads,)), dma((heads,)),
        ] + gather_sems(1, chips),
        compiler_params=pltpu.CompilerParams(
            collective_id=1, has_side_effects=True, vmem_limit_bytes=56 * 1024 * 1024),
        name="tail",
    )(gated, hid, ngain, fgain, out_t, lm_head, ref_logits, tokens, out_t)


def shards(
    groups, heads,
    hidden_in, ssm_state, conv_x_state, conv_bc_state, token_ids, ref_logits,
    in_z, in_x, in_bc, in_dt, out_t, lm_head,
    conv_wx, conv_bx, conv_wbc, conv_bbc, dt_bias, a_log, skip_gain, norm_in, norm_gain, final_gain,
):
    local_heads = a_log.shape[0]
    dt_wide = jnp.pad(in_dt, ((0, 0), (0, -in_dt.shape[1] % 128)))
    roll_bc, dt_all, roll_x, roll_z = gather(groups, [in_bc, dt_wide, in_x, in_z])
    roll_dt = dt_all[:, :local_heads]
    stream_in = hidden_in.astype(jnp.float32)
    normed = rms_norm(stream_in, norm_in).astype(jnp.bfloat16)
    gate_branch = jnp.dot(normed, roll_z, preferred_element_type=jnp.float32).astype(jnp.bfloat16)
    x_branch = jnp.dot(normed, roll_x, preferred_element_type=jnp.float32).astype(jnp.bfloat16)
    bc_branch = jnp.dot(normed, roll_bc, preferred_element_type=jnp.float32).astype(jnp.bfloat16)
    step_raw = jnp.dot(normed, dt_all, preferred_element_type=jnp.float32).astype(jnp.bfloat16)
    step_raw = step_raw[:, :local_heads]
    x_conv = causal_conv(conv_x_state, x_branch, conv_wx, conv_bx)
    bc_conv = causal_conv(conv_bc_state, bc_branch, conv_wbc, conv_bbc)
    state_size = bc_conv.shape[1] // 2
    b_vals = bc_conv[:, :state_size]
    c_vals = bc_conv[:, state_size:]
    step = jax.nn.softplus(step_raw.astype(jnp.float32) + dt_bias)
    decay = jnp.exp(-step * jnp.exp(a_log))
    seqs = x_conv.shape[0]
    inner = local_heads * P_SIZE
    spread = lambda v: jnp.repeat(v, P_SIZE, axis=-1)
    new_state, ssm_out = state_step(
        spread(decay), spread(step) * x_conv, b_vals, c_vals, ssm_state.reshape(seqs, inner, state_size))
    new_state = new_state.reshape(ssm_state.shape)
    ssm_out = ssm_out + spread(skip_gain)[None] * x_conv
    gated = (ssm_out * jax.nn.silu(gate_branch.astype(jnp.float32))).astype(jnp.bfloat16)
    depth = out_t.shape[0]
    extra = -depth % 128 or 128
    hid = hidden_in.reshape(seqs, groups, depth).transpose(1, 0, 2)
    hid = jnp.pad(hid, ((0, 0), (0, 0), (0, extra)))
    fgain = lax.dynamic_slice(final_gain, (lax.axis_index("group") * depth,), (depth,))
    fgain = jnp.pad(fgain, (0, extra))[None]
    roll_out, result = tail(
        groups, heads, gated, hid, norm_gain[None], fgain, out_t, lm_head, ref_logits, token_ids[:, None])
    return (new_state, result[:, 0], result[:, 1], roll_z, roll_x, roll_bc, roll_dt, roll_out)


def solution(mesh):
    return jax.shard_map(
        functools.partial(shards, mesh.shape["group"], mesh.shape["head"]),
        mesh=mesh,
        in_specs=(
            P("group", None),
            P("group", "head", None, None),
            P("group", None, "head"),
            P("group", None, None),
            P("group"),
            P("group", "head"),
            P("group", "head"),
            P("group", "head"),
            P("group", None),
            P("group", "head"),
            P("group", "head"),
            P("head", "group"),
            P(None, "head"),
            P("head"),
            P(),
            P(),
            P("head"),
            P("head"),
            P("head"),
            P(),
            P("head"),
            P(),
        ),
        out_specs=(
            P("group", "head", None, None),
            P("group"),
            P("group"),
            P(None, "head"),
            P(None, "head"),
            P(),
            P(None, "head"),
            P(None, "head"),
        ),
        check_vma=False,
    )
```

time: 325 us -> 203 us (0.62)
  Pallas kernels: 0 us -> 153 us
  blocking collectives: 108 us -> 0 us
  waiting for transfers between devices: 103 us -> 0 us
  matrix products: 43.6 us -> 11.4 us
  between operations: 14.1 us -> 0.83 us
  other arithmetic: 12.4 us -> 1.15 us
  starting transfers between devices: 9.02 us -> 0 us
    pallas_call x0 -> x3, Pallas kernels: none -> 153 us  [the longest x1 70.8 us: gather(): pl.pallas_call(functools.partial(gather_kernel, groups, count), out_shape...]
    all_gather x2 -> x0, blocking collectives: 76.8 us -> none  [the longest x1 66.7 us: shards(): lax.all_gather(in_dt, 'group', axis=0, tiled=True)]
    all_gather x4 -> x0, waiting for transfers between devices: 56.4 us -> none  [the longest x1 32.6 us: shards(): lax.all_gather(out_t, 'group', axis=0, tiled=True)]
    psum x1 -> x0, waiting for transfers between devices: 35 us -> none  [shards(): mixed = lax.psum(partial_mix, 'head')]
    dot_general x4 -> x1, matrix products: 34.1 us -> 1.4 us  [shards(): jnp.dot(normed, dt_all, preferred_element_type=jnp.float32)]
    psum x2 -> x0, blocking collectives: 20.2 us -> none  [the longest x1 11.7 us: shards(): square_total = lax.psum(jnp.sum(gated * gated, axis=-1), 'head')]
    all_to_all x4 -> x0, local copies, waits for them, and re-layouts: 16.1 us -> none  [the longest x2 15.8 us: shards(): lax.all_to_all(lm_head, 'group', split_axis=0, concat_axis=1, tiled=True)]
    pmax x1 -> x0, blocking collectives: 10.6 us -> none  [shards(): lax.pmax((jnp.max(logits, axis=-1), jnp.max(reference_rows, axis=-1)), 'h...]
  transfers between devices with their start and end apart: 7 -> 0, of which waited for: 5 -> 0; matrix products, arithmetic and copies ran while one was open for 17% -> 0% of each run, Pallas kernels for 0% -> 0%
where the time goes in v1:
time: 203 us
  Pallas kernels  153 us (75%)
  local copies, waits for them, and re-layouts  36.8 us (18%)
  matrix products  11.4 us (6%)
    pallas_call x1, Pallas kernels, gather(): pl.pallas_call(functools.partial(gather_kernel, groups, count), out_shape...  70.8 us
    pallas_call x1, Pallas kernels, tail(): pl.pallas_call(functools.partial(tail_kernel, groups, heads, seqs), out_s...  55.4 us
    pallas_call x1, Pallas kernels, state_step(): pl.pallas_call(state_kernel, grid=(seqs,), in_specs=[row(rows), row(rows)...  26.3 us
    unnamed x33, local copies, waits for them, and re-layouts  25.1 us
    dot_general x1, matrix products, shards(): jnp.dot(normed, roll_z, preferred_element_type=jnp.float32)  4.5 us

profile of v1, /device:TPU:0, one launch (start us, length us, event | category | flops | bytes accessed | tf_op | source)
XLA Modules:
  0.0 202.7 jit_solution(16387079930714746926)
XLA Ops:
  0.7 0.7 exp.31
  1.4 1.0 fusion.3
  2.4 0.8 dynamic_slice.3
  3.2 0.6 broadcast_in_dim.47.fgain_ref
  3.7 1.3 broadcast_in_dim.46.ngain_ref
  5.0 1.3 copy.42.token_ref
  6.4 0.7 broadcast_in_dim.45
  7.1 0.1 mul.103
  7.2 0.9 copy.36
  8.0 0.7 pad.12.refs_1_
  8.7 1.0 reshape.96
  9.7 0.7 pad.13.hid_ref
  10.4 7.2 %copy.41.lm_ref = bf16[6400,320]{1,0:T(8,128)(2,1)} copy(bf16[6400,320]{0,1:T(8,128)(2,1)} %param.33) | data formatting | bytes 8192000 | tf_op args[11]
  17.6 70.8 %gather_in.1 = (bf16[2560,256]{1,0:T(8,128)(2,1)}, bf16[2560,128]{1,0:T(8,128)(2,1)}, bf16[2560,1280]{1,0:T(8,128)(2,1)}, bf16[2560,1280]{1,0:T(8,128)(2,1)}) custom-call(bf16[320,256]{1,0:T(8,128)(2,1)} %refs_0_.1, bf16[320,128]{1,0:T(8,128)(2,1)} %pad.12.refs_1_, bf16[320,1280]{1,0:T(8,128)(2,1)} %refs_2_.1, bf16[320,1280]{1,0:T(8,128)(2,1)} %refs_3_.1), custom_call_target="tpu_custom_call" | custom-call | tf_op jit(solution)/shard_map/gather_in/pallas_call | solution.py:147
  88.4 1.4 fusion.11
  89.8 1.6 fusion.2
  91.5 0.6 fusion.13
  92.1 3.9 %fusion.1 = bf16[16,1,1280]{2,0,1:T(8,128)(2,1)S(1)} fusion(bf16[2560,1280]{1,0:T(8,128)(2,1)} %get-tuple-element.58, bf16[16,2560]{1,0:T(8,128)(2,1)S(1)} %copy-done.1, f32[2560]{0:T(1024)S(1)} %copy-done.3, f32[16]{0:T(128)S(1)} %add_rsqrt_fusion), kind=kOutput, calls=%fused_computation.3 | convolution fusion | flops 105041920 | bytes 6686784 | tf_op jit(solution)/shard_map/dot_general | solution.py:398
  96.1 0.9 copy.43
  97.0 0.1 broadcast_in_dim.39
  97.1 0.8 broadcast_in_dim_reshape.5.decay_ref
  97.9 0.1 broadcast_in_dim.40
  98.0 0.1 reshape.93
  98.2 0.7 copy.38.inflow_ref
  98.9 26.3 %state_step.1 = (f32[16,1280,128]{2,1,0:T(8,128)}, f32[16,1,1280]{2,1,0:T(1,128)}) custom-call(f32[16,1,1280]{2,1,0:T(1,128)} %broadcast_in_dim_reshape.5.decay_ref, f32[16,1,1280]{2,1,0:T(1,128)} %copy.38.inflow_ref, f32[16,1,128]{2,1,0:T(1,128)} %bitcast.35, f32[16,1,128]{2,1,0:T(1,128)} %bitcast.34, f32[16,1280,128]{2,1,0:T(8,128)} %bitcast.31), custom_call_target="tpu_custom_call" | custom-call | tf_op jit(solution)/shard_map/state_step/pallas_call | solution.py:181
  125.2 4.5 %fusion.7.gated_ref = bf16[16,1280]{1,0:T(8,128)(2,1)} fusion(f32[16,1,1280]{2,1,0:T(1,128)} %get-tuple-element.20, bf16[2560,1280]{1,0:T(8,128)(2,1)} %get-tuple-element.57, f32[16,1280]{1,0:T(8,128)S(1)} %multiply_reduce_fusion, f32[1280]{0:T(1024)S(1)} %copy-done.5, f32[1280]{0:T(1024)S(1)} %mul.103, bf16[16,2560]{1,0:T(8,128)(2,1)S(1)} %copy-done.1, ...), kind=kOutput, calls=%fused_computation.15 | convolution fusion | flops 105328640 | bytes 6860864 | tf_op jit(solution)/shard_map/dot_general | solution.py:397
  129.7 55.4 %tail.1 = (bf16[2560,1280]{1,0:T(8,128)(2,1)}, f32[16,128]{1,0:T(8,128)}) custom-call(bf16[16,1280]{1,0:T(8,128)(2,1)} %fusion.7.gated_ref, bf16[8,16,384]{2,1,0:T(8,128)(2,1)} %pad.13.hid_ref, f32[1,1280]{1,0:T(1,128)} %broadcast_in_dim.46.ngain_ref, f32[1,384]{1,0:T(1,128)} %broadcast_in_dim.47.fgain_ref, bf16[320,1280]{1,0:T(8,128)(2,1)} %out_hbm.1, ...), custom_call_target="tpu_custom_call" | custom-call | tf_op jit(solution)/shard_map/tail/pallas_call | solution.py:360
  185.1 1.5 slice_reduce_fusion
  186.6 6.2 %copy.52 = bf16[2560,1280]{1,0:T(8,128)(2,1)} copy(bf16[2560,1280]{1,0:T(8,128)(2,1)} %get-tuple-element.57) | data formatting | bytes 13107200
  192.8 2.8 %copy.53 = bf16[2560,1280]{1,0:T(8,128)(2,1)} copy(bf16[2560,1280]{1,0:T(8,128)(2,1)S(1)} %bitcast.30) | data formatting | bytes 13107200
  195.6 1.1 copy.54
  196.7 6.1 %copy.55 = bf16[2560,1280]{1,0:T(8,128)(2,1)} copy(bf16[2560,1280]{1,0:T(8,128)(2,1)} %get-tuple-element.61) | data formatting | bytes 13107200
  (35 shorter events, 0.2 us)
Async XLA Ops:
  0.6 87.7 %copy-start.1 = (bf16[16,2560]{1,0:T(8,128)(2,1)S(1)}, bf16[16,2560]{1,0:T(8,128)(2,1)}, u32[]{:S(2)}) copy-start(bf16[16,2560]{1,0:T(8,128)(2,1)} %param.22) | copy-start | bytes 245764
  0.6 87.7 %copy-start.3 = (f32[2560]{0:T(1024)S(1)}, f32[2560]{0:T(1024)}, u32[]{:S(2)}) copy-start(f32[2560]{0:T(1024)} %param.41) | copy-start | bytes 30724
  10.4 81.1 %copy-start.6 = (bf16[16,3,256]{2,0,1:T(8,128)(2,1)S(1)}, bf16[16,3,256]{2,0,1:T(8,128)(2,1)}, u32[]{:S(2)}) copy-start(bf16[16,3,256]{2,0,1:T(8,128)(2,1)} %param.25) | copy-start | bytes 73732
  10.4 81.1 %copy-start.8 = (f32[4,256]{1,0:T(4,128)S(1)}, f32[4,256]{1,0:T(4,128)}, u32[]{:S(2)}) copy-start(f32[4,256]{1,0:T(4,128)} %param.36) | copy-start | bytes 12292
  10.4 81.1 %copy-start.9 = (f32[256]{0:T(256)S(1)}, f32[256]{0:T(256)}, u32[]{:S(2)}) copy-start(f32[256]{0:T(256)} %param.37) | copy-start | bytes 3076
  10.4 81.7 %copy-start.10 = (f32[20]{0:T(128)S(1)}, f32[20]{0:T(128)}, u32[]{:S(2)}) copy-start(f32[20]{0:T(128)} %param.38) | copy-start | bytes 244
  17.6 78.4 %copy-start.4 = (bf16[16,3,1280]{2,0,1:T(8,128)(2,1)S(1)}, bf16[16,3,1280]{2,0,1:T(8,128)(2,1)}, u32[]{:S(2)}) copy-start(bf16[16,3,1280]{2,0,1:T(8,128)(2,1)} %param.24) | copy-start | bytes 368644
  17.6 78.4 %copy-start.7 = (f32[4,1280]{1,0:T(4,128)S(1)}, f32[4,1280]{1,0:T(4,128)}, u32[]{:S(2)}) copy-start(f32[4,1280]{1,0:T(4,128)} %param.34) | copy-start | bytes 61444
  17.6 80.5 %copy-start.5 = (f32[1280]{0:T(1024)S(1)}, f32[1280]{0:T(1024)}, u32[]{:S(2)}) copy-start(f32[1280]{0:T(1024)} %param.35) | copy-start | bytes 15364
  88.4 7.7 %copy-start.2 = (bf16[2560,128]{1,0:T(8,128)(2,1)S(1)}, bf16[2560,128]{1,0:T(8,128)(2,1)}, u32[]{:S(2)}) copy-start(bf16[2560,128]{1,0:T(8,128)(2,1)} %get-tuple-element.16) | copy-start | bytes 1966084
  129.7 63.1 %slice-start = ((s8[6553600]{0:T(1024)(128)(4,1)}), s8[2359296]{0:T(1024)(128)(4,1)S(1)}, s32[]{:S(2)}) async-start(s8[6553600]{0:T(1024)(128)(4,1)} %bitcast.29), calls=%async_computation | async-start | bytes 4718592
  186.6 6.2 %slice-start.1 = ((s8[6553600]{0:T(1024)(128)(4,1)}), s8[4194304]{0:T(1024)(128)(4,1)S(1)}, s32[]{:S(2)}) async-start(s8[6553600]{0:T(1024)(128)(4,1)} %bitcast.29), calls=%async_computation.1 | async-start | bytes 8388608
  192.8 2.8 %copy-start = (bf16[2560,256]{1,0:T(8,128)(2,1)S(1)}, bf16[2560,256]{1,0:T(8,128)(2,1)}, u32[]{:S(2)}) copy-start(bf16[2560,256]{1,0:T(8,128)(2,1)} %get-tuple-element.59) | copy-start | bytes 3932164

commit v2 on v1

--- a/solution.py
+++ b/solution.py
@@ -155,38 +155,85 @@
     )(*arrays)
 
 
-def state_kernel(decay_ref, inflow_ref, b_ref, c_ref, state_ref, new_ref, y_ref):
-    def column(row, other):
-        first = lax.broadcasted_iota(jnp.int32, (8, row.shape[1]), 0) == 0
-        left = jnp.where(first, jnp.broadcast_to(row, (8, row.shape[1])), 0.0)
-        right = jnp.broadcast_to(other, (8, other.shape[1]))
-        return lax.dot_general(
-            left, right, (((0,), (0,)), ((), ())),
-            precision=lax.Precision.HIGHEST, preferred_element_type=jnp.float32)
-
-    b = b_ref[0]
-    decay = column(decay_ref[0], jnp.ones_like(b))
-    new = decay * state_ref[0] + column(inflow_ref[0], b)
-    new_ref[0] = new
-    c = jnp.broadcast_to(c_ref[0], (16, b.shape[1])).astype(jnp.bfloat16)
-    y = lax.dot_general(
-        c, new.astype(jnp.bfloat16), (((1,), (1,)), ((), ())), preferred_element_type=jnp.float32)
-    y_ref[0] = y[0:1]
+def project_kernel(steps, normed_ref, *refs):
+    count = len(refs) // 4
+    weights, sums, copies, totals = (refs[n * count:(n + 1) * count] for n in range(4))
+    step = pl.program_id(0)
+
+    @pl.when(step == 0)
+    def _():
+        for total in totals:
+            total[...] = jnp.zeros_like(total)
+
+    for weight, copied, total in zip(weights, copies, totals):
+        block = weight[...]
+        copied[...] = block
+        total[...] += jnp.dot(normed_ref[...], block, preferred_element_type=jnp.float32)
+
+    @pl.when(step == steps - 1)
+    def _():
+        for out, total in zip(sums, totals):
+            out[...] = total[...].astype(out.dtype)
+
+
+def project(normed, weights):
+    seqs, depth = normed.shape
+    steps = 5
+    rows = depth // steps
+    whole = lambda w: pl.BlockSpec((seqs, w.shape[1]), lambda k: (0, 0))
+    block = lambda w: pl.BlockSpec((rows, w.shape[1]), lambda k: (k, 0))
+    made = pl.pallas_call(
+        functools.partial(project_kernel, steps),
+        grid=(steps,),
+        in_specs=[pl.BlockSpec((seqs, rows), lambda k: (0, k))] + [block(w) for w in weights],
+        out_specs=[whole(w) for w in weights] + [block(w) for w in weights],
+        out_shape=[jax.ShapeDtypeStruct((seqs, w.shape[1]), jnp.bfloat16) for w in weights]
+        + [jax.ShapeDtypeStruct(w.shape, w.dtype) for w in weights],
+        scratch_shapes=[pltpu.VMEM((seqs, w.shape[1]), jnp.float32) for w in weights],
+        name="project",
+    )(normed, *weights)
+    return made[:len(weights)], made[len(weights):]
+
+
+def state_kernel(each, decay_ref, inflow_ref, b_ref, c_ref, state_ref, new_ref, y_ref):
+    heads, width, size = state_ref.shape[1:]
+
+    def pair(row):
+        high = row.astype(jnp.bfloat16).astype(jnp.float32)
+        return high, row - high
+
+    for n in range(each):
+        seq = pl.program_id(0) * each + n
+        high, low = pair(inflow_ref[n])
+        b_high, b_low = pair(b_ref[n])
+        place = lax.broadcasted_iota(jnp.int32, (16, heads * width), 0)
+        left = jnp.where(place < 2, high, jnp.where(place < 4, low, 0.0)).astype(jnp.bfloat16)
+        place = lax.broadcasted_iota(jnp.int32, (16, size), 0)
+        right = jnp.where(place % 2 == 0, b_high, b_low).astype(jnp.bfloat16)
+        inflow = lax.dot_general(
+            left, right, (((0,), (0,)), ((), ())), preferred_element_type=jnp.float32)
+        for h in range(heads):
+            new_ref[n, h] = decay_ref[seq, h] * state_ref[n, h] + inflow[h * width:(h + 1) * width]
+        new = new_ref[n].reshape(heads * width, size).astype(jnp.bfloat16)
+        c = jnp.broadcast_to(c_ref[n], (16, size)).astype(jnp.bfloat16)
+        y = lax.dot_general(c, new, (((1,), (1,)), ((), ())), preferred_element_type=jnp.float32)
+        y_ref[n] = y[0:1]
 
 
 def state_step(decay, inflow, b_vals, c_vals, state):
-    seqs, rows, size = state.shape
-    row = lambda width: pl.BlockSpec((1, 1, width), lambda s: (s, 0, 0))
-    block = pl.BlockSpec((1, rows, size), lambda s: (s, 0, 0))
+    seqs, heads, width, size = state.shape
+    each = 2
+    row = lambda wide: pl.BlockSpec((each, 1, wide), lambda s: (s, 0, 0))
+    block = pl.BlockSpec((each, heads, width, size), lambda s: (s, 0, 0, 0))
     new, y = pl.pallas_call(
-        state_kernel,
-        grid=(seqs,),
-        in_specs=[row(rows), row(rows), row(size), row(size), block],
-        out_specs=[block, row(rows)],
+        functools.partial(state_kernel, each),
+        grid=(seqs // each,),
+        in_specs=[pl.BlockSpec(memory_space=pltpu.SMEM), row(heads * width), row(size), row(size), block],
+        out_specs=[block, row(heads * width)],
         out_shape=[jax.ShapeDtypeStruct(state.shape, jnp.float32),
-                   jax.ShapeDtypeStruct((seqs, 1, rows), jnp.float32)],
+                   jax.ShapeDtypeStruct((seqs, 1, heads * width), jnp.float32)],
         name="state_step",
-    )(decay[:, None], inflow[:, None], b_vals[:, None], c_vals[:, None], state)
+    )(decay, inflow[:, None], b_vals[:, None], c_vals[:, None], state)
     return new, y[:, 0]
 
 
@@ -199,7 +246,7 @@
     groups, heads, seqs,
     gated_ref, hid_ref, ngain_ref, fgain_ref, out_t_ref, lm_ref, refl_ref, token_ref, out_hbm,
     roll_out, result_ref,
-    gall, hall, mix, pairs, pair_in, sums, sums_in, stat,
+    gall, hall, mix, pairs, pair_in, sums, sums_in, square, square_in, squares_out, squares_in, stat,
     gsend, grecv, hsend, hrecv, msend, mrecv, psend, precv, ssend, srecv, tsend, trecv,
     *gsems,
 ):
@@ -208,7 +255,9 @@
     chip, core = group // 2, group % 2
     wide = mix.shape[2]
     depth = out_t_ref.shape[0]
-    vocab = lm_ref.shape[0]
+    vocab = lm_ref.shape[1]
+    parts = pairs.shape[0]
+    width = vocab // parts
     rows = groups * seqs
     pending = []
 
@@ -270,39 +319,49 @@
     tail_lanes = lax.broadcasted_iota(jnp.int32, (rows, 128), 1)
     packed = halves(final_squares, tail_lanes, 0, 64).astype(jnp.bfloat16)
     half = chips * seqs
-    for side in (0, 1):
-        pairs[side, :, vocab:vocab + 128] = packed[side * half:(side + 1) * half]
-    step_width = 640
-
-    @pl.loop(0, vocab // step_width)
-    def _(t):
-        at = pl.ds(pl.multiple_of(t * step_width, step_width), step_width)
+    other = {"group": chip * 2 + 1 - core}
+    square[0], square[1] = packed[:half], packed[half:]
+    pair_sends = [send(square.at[1 - core], square_in, other, psend.at[parts], precv.at[parts])]
+    last = []
+
+    def out(source, target, t):
+        for m in range(1, chips):
+            peer = flip(chip, m)
+            last.append(send(
+                source.at[peer], target.at[m], {"group": peer * 2 + core}, ssend.at[t, m], srecv.at[t, m]))
+        target[0] = source[chip]
+
+    def join(t):
+        pair_sends[t + 1].wait_recv()
+        joined = pairs[t, core].astype(jnp.float32) + pair_in[t].astype(jnp.float32)
+        sums[t] = joined.astype(jnp.bfloat16).reshape(chips, seqs, width)
+        out(sums.at[t], sums_in.at[t], t)
+
+    for t in range(parts):
         block = lax.dot_general(
-            final, lm_ref[at, :], (((1,), (1,)), ((), ())), preferred_element_type=jnp.float32)
-        block = block.astype(jnp.bfloat16)
-        pairs[0, :, at] = block[:half]
-        pairs[1, :, at] = block[half:]
-
-    pair = send(pairs.at[1 - core], pair_in, {"group": chip * 2 + 1 - core}, psend, precv)
-    pair.wait_recv()
-    joined = pairs[core].astype(jnp.float32) + pair_in[...].astype(jnp.float32)
-    sums[:, :, :vocab] = joined[:, :vocab].astype(jnp.bfloat16).reshape(chips, seqs, vocab)
-    rest = joined[:, vocab:]
-    rest = rest[:, 0:1] + rest[:, 64:65]
-    packed = halves(rest, lax.broadcasted_iota(jnp.int32, (half, 128), 1), 0, 64)
-    sums[:, :, vocab:] = packed.astype(jnp.bfloat16).reshape(chips, seqs, 128)
-    last = []
-    for m in range(1, chips):
-        peer = flip(chip, m)
-        last.append(send(sums.at[peer], sums_in.at[m], {"group": peer * 2 + core}, ssend.at[m], srecv.at[m]))
-    sums_in[0] = sums[chip]
+            final, lm_ref[:, t * width:(t + 1) * width], (((1,), (0,)), ((), ())),
+            preferred_element_type=jnp.float32).astype(jnp.bfloat16)
+        pairs[t, 0], pairs[t, 1] = block[:half], block[half:]
+        pair_sends.append(send(pairs.at[t, 1 - core], pair_in.at[t], other, psend.at[t], precv.at[t]))
+        if t == 0:
+            pair_sends[0].wait_recv()
+            rest = square[core].astype(jnp.float32) + square_in[...].astype(jnp.float32)
+            rest = rest[:, 0:1] + rest[:, 64:65]
+            split = halves(rest, lax.broadcasted_iota(jnp.int32, (half, 128), 1), 0, 64)
+            squares_out[...] = split.astype(jnp.bfloat16).reshape(chips, seqs, 128)
+            out(squares_out, squares_in, parts)
+        else:
+            join(t - 1)
+    join(parts - 1)
     work.relay_far(0)
     for made in last:
         made.wait_recv()
 
-    logits = jnp.sum(sums_in[...].astype(jnp.float32), axis=0)
-    mean_square = (logits[:, vocab:vocab + 1] + logits[:, vocab + 64:vocab + 65]) / (depth * groups)
-    logits = logits[:, :vocab] * lax.rsqrt(mean_square + EPSILON)
+    square_sum = jnp.sum(squares_in[...].astype(jnp.float32), axis=0)
+    mean_square = (square_sum[:, 0:1] + square_sum[:, 64:65]) / (depth * groups)
+    logits = jnp.concatenate(
+        [jnp.sum(sums_in[t].astype(jnp.float32), axis=0) for t in range(parts)], axis=1)
+    logits = logits * lax.rsqrt(mean_square + EPSILON)
     reference = refl_ref[...].astype(jnp.float32)
     columns = lax.broadcasted_iota(jnp.int32, (seqs, vocab), 1) + head * vocab
     picked = jnp.sum(jnp.where(columns == token_ref[...], logits, 0.0), axis=-1, keepdims=True)
@@ -352,7 +411,9 @@
     seqs, inner = gated.shape
     depth = out_t.shape[0]
     wide = hid.shape[2]
-    vocab = lm_head.shape[0]
+    vocab = lm_head.shape[1]
+    parts = 5
+    width = vocab // parts
     chips = groups // 2
     vmem, any_spec = pl.BlockSpec(memory_space=pltpu.VMEM), pl.BlockSpec(memory_space=pl.ANY)
     dma = pltpu.SemaphoreType.DMA
@@ -367,14 +428,18 @@
             pltpu.VMEM((groups, seqs, inner), bf16),
             pltpu.VMEM((groups, seqs, wide), bf16),
             pltpu.VMEM((heads, groups * seqs, wide), bf16),
-            pltpu.VMEM((2, chips * seqs, vocab + 128), bf16),
-            pltpu.VMEM((chips * seqs, vocab + 128), bf16),
-            pltpu.VMEM((chips, seqs, vocab + 128), bf16),
-            pltpu.VMEM((chips, seqs, vocab + 128), bf16),
+            pltpu.VMEM((parts, 2, chips * seqs, width), bf16),
+            pltpu.VMEM((parts, chips * seqs, width), bf16),
+            pltpu.VMEM((parts, chips, seqs, width), bf16),
+            pltpu.VMEM((parts, chips, seqs, width), bf16),
+            pltpu.VMEM((2, chips * seqs, 128), bf16),
+            pltpu.VMEM((chips * seqs, 128), bf16),
+            pltpu.VMEM((chips, seqs, 128), bf16),
+            pltpu.VMEM((chips, seqs, 128), bf16),
             pltpu.VMEM((heads, seqs, 128), jnp.float32),
             dma((groups,)), dma((groups,)), dma((groups,)), dma((groups,)),
-            dma((heads,)), dma((heads,)), dma, dma,
-            dma((chips,)), dma((chips,)), dma((heads,)), dma((heads,)),
+            dma((heads,)), dma((heads,)), dma((parts + 1,)), dma((parts + 1,)),
+            dma((parts + 1, chips)), dma((parts + 1, chips)), dma((heads,)), dma((heads,)),
         ] + gather_sems(1, chips),
         compiler_params=pltpu.CompilerParams(
             collective_id=1, has_side_effects=True, vmem_limit_bytes=56 * 1024 * 1024),
@@ -391,13 +456,11 @@
     local_heads = a_log.shape[0]
     dt_wide = jnp.pad(in_dt, ((0, 0), (0, -in_dt.shape[1] % 128)))
     roll_bc, dt_all, roll_x, roll_z = gather(groups, [in_bc, dt_wide, in_x, in_z])
-    roll_dt = dt_all[:, :local_heads]
     stream_in = hidden_in.astype(jnp.float32)
     normed = rms_norm(stream_in, norm_in).astype(jnp.bfloat16)
-    gate_branch = jnp.dot(normed, roll_z, preferred_element_type=jnp.float32).astype(jnp.bfloat16)
-    x_branch = jnp.dot(normed, roll_x, preferred_element_type=jnp.float32).astype(jnp.bfloat16)
-    bc_branch = jnp.dot(normed, roll_bc, preferred_element_type=jnp.float32).astype(jnp.bfloat16)
-    step_raw = jnp.dot(normed, dt_all, preferred_element_type=jnp.float32).astype(jnp.bfloat16)
+    (gate_branch, x_branch, bc_branch, step_raw), (roll_z, roll_x, roll_bc, dt_all) = project(
+        normed, (roll_z, roll_x, roll_bc, dt_all))
+    roll_dt = dt_all[:, :local_heads]
     step_raw = step_raw[:, :local_heads]
     x_conv = causal_conv(conv_x_state, x_branch, conv_wx, conv_bx)
     bc_conv = causal_conv(conv_bc_state, bc_branch, conv_wbc, conv_bbc)
@@ -407,11 +470,9 @@
     step = jax.nn.softplus(step_raw.astype(jnp.float32) + dt_bias)
     decay = jnp.exp(-step * jnp.exp(a_log))
     seqs = x_conv.shape[0]
-    inner = local_heads * P_SIZE
     spread = lambda v: jnp.repeat(v, P_SIZE, axis=-1)
     new_state, ssm_out = state_step(
-        spread(decay), spread(step) * x_conv, b_vals, c_vals, ssm_state.reshape(seqs, inner, state_size))
-    new_state = new_state.reshape(ssm_state.shape)
+        decay, spread(step) * x_conv, b_vals, c_vals, ssm_state)
     ssm_out = ssm_out + spread(skip_gain)[None] * x_conv
     gated = (ssm_out * jax.nn.silu(gate_branch.astype(jnp.float32))).astype(jnp.bfloat16)
     depth = out_t.shape[0]
@@ -421,7 +482,7 @@
     fgain = lax.dynamic_slice(final_gain, (lax.axis_index("group") * depth,), (depth,))
     fgain = jnp.pad(fgain, (0, extra))[None]
     roll_out, result = tail(
-        groups, heads, gated, hid, norm_gain[None], fgain, out_t, lm_head, ref_logits, token_ids[:, None])
+        groups, heads, gated, hid, norm_gain[None], fgain, out_t, lm_head.T, ref_logits, token_ids[:, None])
     return (new_state, result[:, 0], result[:, 1], roll_z, roll_x, roll_bc, roll_dt, roll_out)
 
 

time: 203 us -> 180 us (0.89)
  local copies, waits for them, and re-layouts: 36.8 us -> 19.8 us
  matrix products: 11.4 us -> 0 us
  other arithmetic: 1.15 us -> 7.09 us
    unnamed x33 -> x19, local copies, waits for them, and re-layouts: 25.1 us -> 8.98 us
    dot_general x4 -> x0, matrix products: 11.4 us -> none  [the longest x1 4.5 us: shards(): jnp.dot(normed, roll_z, preferred_element_type=jnp.float32)]
    convert_element_type x0 -> x2, other arithmetic: none -> 3.18 us  [the longest x1 1.61 us: shards(): normed = rms_norm(stream_in, norm_in).astype(jnp.bfloat16)]
    pallas_call x1 -> x2, Pallas kernels: 26.3 us -> 25.5 us  [the longest x1 13.3 us: project(): pl.pallas_call(functools.partial(project_kernel, steps), grid=(steps,), i...]
where the time goes in v2:
time: 180 us; the launch traced here: 179 us
  Pallas kernels  152 us (84%)
  local copies, waits for them, and re-layouts  19.8 us (11%)
  other arithmetic  7.09 us (4%)
    pallas_call x1, Pallas kernels, gather(): pl.pallas_call(functools.partial(gather_kernel, groups, count), out_shape...  70.7 us
    pallas_call x1, Pallas kernels, tail(): pl.pallas_call(functools.partial(tail_kernel, groups, heads, seqs), out_s...  55.5 us
    pallas_call x1, Pallas kernels, project(): pl.pallas_call(functools.partial(project_kernel, steps), grid=(steps,), i...  13.3 us
    pallas_call x1, Pallas kernels, state_step(): pl.pallas_call(functools.partial(state_kernel, each), grid=(seqs // each,...  12.2 us
    unnamed x19, local copies, waits for them, and re-layouts  8.98 us

profile of v2, /device:TPU:0, one launch (start us, length us, event | category | flops | bytes accessed | tf_op | source)
XLA Modules:
  0.0 179.4 jit_solution(5700333840193086981)
XLA Ops:
  0.6 0.7 exp.31
  1.3 1.0 fusion
  2.3 0.8 dynamic_slice.3
  3.1 0.6 broadcast_in_dim.43.fgain_ref
  3.7 1.3 broadcast_in_dim.42.ngain_ref
  5.0 1.3 copy.39.token_ref
  6.3 0.7 broadcast_in_dim.41
  7.1 0.1 mul.103
  7.1 1.6 fusion.2.normed_ref
  8.7 0.9 copy.35
  9.6 0.7 pad.12.refs_1_
  10.2 1.0 reshape.88
  11.3 0.7 pad.13.hid_ref
  11.9 70.7 %gather_in.1 = (bf16[2560,256]{1,0:T(8,128)(2,1)}, bf16[2560,128]{1,0:T(8,128)(2,1)}, bf16[2560,1280]{1,0:T(8,128)(2,1)}, bf16[2560,1280]{1,0:T(8,128)(2,1)}) custom-call(bf16[320,256]{1,0:T(8,128)(2,1)} %refs_0_.1, bf16[320,128]{1,0:T(8,128)(2,1)} %pad.12.refs_1_, bf16[320,1280]{1,0:T(8,128)(2,1)} %refs_2_.1, bf16[320,1280]{1,0:T(8,128)(2,1)} %refs_3_.1), custom_call_target="tpu_custom_call" | custom-call | tf_op jit(solution)/shard_map/gather_in/pallas_call | solution.py:147
  82.7 0.0 copy-start.7
  82.7 0.0 copy-start.3
  82.7 0.0 copy-start.6
  82.7 0.0 copy-start
  82.7 13.3 %project.1 = (bf16[16,1280]{1,0:T(8,128)(2,1)}, bf16[16,1280]{1,0:T(8,128)(2,1)}, bf16[16,256]{1,0:T(8,128)(2,1)}, bf16[16,128]{1,0:T(8,128)(2,1)}, bf16[2560,12...) custom-call(bf16[16,2560]{1,0:T(8,128)(2,1)} %fusion.2.normed_ref, ...), custom_call_target="tpu_custom_call" | custom-call | tf_op jit(solution)/shard_map/project/pallas_call | solution.py:185
  96.1 1.3 compare_select_fusion
  97.4 0.7 multiply_reduce_fusion.1
  98.1 0.6 fusion.8
  98.7 0.8 multiply_reduce_fusion
  99.6 2.0 %copy.40 = bf16[2560,20]{0,1:T(8,128)(2,1)} copy(bf16[2560,20]{1,0:T(8,128)(2,1)} %bitcast.23) | data formatting | bytes 204800
  101.6 0.1 broadcast_in_dim.36
  101.7 0.1 reshape.87
  101.8 0.7 copy.36.inflow_ref
  102.6 12.2 %state_step.1 = (f32[16,20,64,128]{3,2,1,0:T(8,128)}, f32[16,1,1280]{2,1,0:T(1,128)}) custom-call(f32[16,20]{1,0:T(8,128)} %get-tuple-element.61.decay_ref, f32[16,1,1280]{2,1,0:T(1,128)} %copy.36.inflow_ref, f32[16,1,128]{2,1,0:T(1,128)} %bitcast.27, f32[16,1,128]{2,1,0:T(1,128)} %bitcast.26, f32[16,20,64,128]{3,2,1,0:T(8,128)} %state_ref.1), custom_call_target="tpu_custom_call" | custom-call | tf_op jit(solution)/shard_map/state_step/pallas_call | solution.py:228
  114.7 1.6 fusion.7.gated_ref
  116.3 55.5 %tail.1 = (bf16[2560,1280]{1,0:T(8,128)(2,1)}, f32[16,128]{1,0:T(8,128)}) custom-call(bf16[16,1280]{1,0:T(8,128)(2,1)} %fusion.7.gated_ref, bf16[8,16,384]{2,1,0:T(8,128)(2,1)} %pad.13.hid_ref, f32[1,1280]{1,0:T(1,128)} %broadcast_in_dim.42.ngain_ref, f32[1,384]{1,0:T(1,128)} %broadcast_in_dim.43.fgain_ref, bf16[320,1280]{1,0:T(8,128)(2,1)} %out_hbm.1, ...), custom_call_target="tpu_custom_call" | custom-call | tf_op jit(solution)/shard_map/tail/pallas_call | solution.py:421
  171.8 1.5 slice_reduce_fusion
  173.3 6.1 %copy.48 = bf16[2560,1280]{1,0:T(8,128)(2,1)} copy(bf16[2560,1280]{1,0:T(8,128)(2,1)} %get-tuple-element.77) | data formatting | bytes 13107200
  (17 shorter events, 0.1 us)
Async XLA Ops:
  82.7 13.4 %copy-start.7 = (f32[20]{0:T(128)S(1)}, f32[20]{0:T(128)}, u32[]{:S(2)}) copy-start(f32[20]{0:T(128)} %param.38) | copy-start | bytes 244
  82.7 14.7 %copy-start.3 = (bf16[16,3,256]{2,0,1:T(8,128)(2,1)S(1)}, bf16[16,3,256]{2,0,1:T(8,128)(2,1)}, u32[]{:S(2)}) copy-start(bf16[16,3,256]{2,0,1:T(8,128)(2,1)} %param.25) | copy-start | bytes 73732
  82.7 14.7 %copy-start.5 = (f32[4,256]{1,0:T(4,128)S(1)}, f32[4,256]{1,0:T(4,128)}, u32[]{:S(2)}) copy-start(f32[4,256]{1,0:T(4,128)} %param.36) | copy-start | bytes 12292
  82.7 15.4 %copy-start.6 = (f32[256]{0:T(256)S(1)}, f32[256]{0:T(256)}, u32[]{:S(2)}) copy-start(f32[256]{0:T(256)} %param.37) | copy-start | bytes 3076
  82.7 16.0 %copy-start = (bf16[16,3,1280]{2,0,1:T(8,128)(2,1)S(1)}, bf16[16,3,1280]{2,0,1:T(8,128)(2,1)}, u32[]{:S(2)}) copy-start(bf16[16,3,1280]{2,0,1:T(8,128)(2,1)} %param.24) | copy-start | bytes 368644
  82.7 16.0 %copy-start.4 = (f32[4,1280]{1,0:T(4,128)S(1)}, f32[4,1280]{1,0:T(4,128)}, u32[]{:S(2)}) copy-start(f32[4,1280]{1,0:T(4,128)} %param.34) | copy-start | bytes 61444
  82.7 19.0 %copy-start.2 = (f32[1280]{0:T(1024)S(1)}, f32[1280]{0:T(1024)}, u32[]{:S(2)}) copy-start(f32[1280]{0:T(1024)} %param.35) | copy-start | bytes 15364
  96.0 18.7 %copy-start.1 = (bf16[16,1280]{1,0:T(8,128)(2,1)S(1)}, bf16[16,1280]{1,0:T(8,128)(2,1)}, u32[]{:S(2)}) copy-start(bf16[16,1280]{1,0:T(8,128)(2,1)} %get-tuple-element.33) | copy-start | bytes 122884
